TPU v7x, 256 devices: a 8x8x2 block of a 8x8x16 slice. The times are simulated.
256 devices in a mesh: groups: 2 (over z), seq: 16 (over y, core), head: 8 (over x).
Axes of the slice: x: 8, y: 8, z: 2, core: 2. Of those that a mesh axis runs over, the one named last changes fastest.
The devices are a block of a 8x8x16 slice.
Arguments:
- queries: bfloat16 [4096, 8192], P(('groups', 'seq'), 'head'), parts along dimension 0
- new_keys: bfloat16 [4096, 1024], P(('groups', 'seq'), 'head'), parts along dimension 0, may hold values from -6 to 6
- new_values: bfloat16 [4096, 1024], P(('groups', 'seq'), 'head'), parts along dimension 0, may hold values from -6 to 6
- cache_keys: bfloat16 [32768, 1024], P(('groups', 'seq'), 'head'), parts along dimension 0
- cache_values: bfloat16 [32768, 1024], P(('groups', 'seq'), 'head'), parts along dimension 0, may hold values from -6 to 6
- valid_len: int32 [32], P('groups'), parts along dimension 0, may hold values from 1 to 1024, as said below
- block_of: int32 [32], P('groups'), parts along dimension 0, may hold values from 0 to 15, each once
Outputs:
- attended: bfloat16 [4096, 8192], P(('groups', 'seq'), 'head'), parts along dimension 0
There are 2 independent parts, one for each index of `groups`. A program takes and returns all parts, laid end to end along the dimension named above; each array names one. Nothing has to cross between parts.
Inputs may be any that keep to these rules, and one draw needn't show every extreme that they name: `valid_len`: some shard is full (1024 filled slots) in every draw; slot 0 of every shard is filled. `block_of`: A permutation of the 16 span blocks.
All inputs are finite; a program needn't handle non-finite values.
Results may differ from a plain program's by a relative error of at most 0.0027.
Values may be sent and summed in bfloat16 or wider, within the bound.
No kernel may reach another device: no remote copies, remote signals or barrier semaphores. Data moves between devices by JAX's collectives and lax.ppermute only.
A program may use at most 192 MiB of HBM per device.

v0:
```python
import jax
import jax.numpy as jnp
from jax import lax
from jax.sharding import PartitionSpec as P

DH = 128
GROUP = 8
NEGATIVE = -1e30


def in_order(tiles, dim):
    shape = list(tiles.shape[1:])
    shape[dim] *= tiles.shape[0]
    return jnp.moveaxis(tiles, 0, dim).reshape(shape)


def from_everyone(array, axis):
    size = lax.axis_size(axis)
    return lax.all_to_all(
        jnp.broadcast_to(array[None], (size, *array.shape)), axis, 0, 0, tiled=True
    )


def gather_directly(array, axis, dim):
    return in_order(from_everyone(array, axis), dim)


def sent_together(arrays, axis, dim, along):
    both = jnp.concatenate(arrays, axis=along)
    filled, at, done = (gather_directly(both, axis, dim), 0, [])
    for a in arrays:
        done.append(lax.slice_in_dim(filled, at, at + a.shape[along], axis=along))
        at += a.shape[along]
    return tuple(done)


def lookup(table, where_at):
    picked = where_at[:, None] == jnp.arange(table.shape[0], dtype=jnp.int32)[None, :]
    return jnp.sum(jnp.where(picked, table[None, :], 0), axis=1)


def scores_of(query_rows, key_rows):
    heads = key_rows.shape[1] // DH
    query_four = query_rows.reshape(query_rows.shape[0], heads, GROUP, DH)
    key_three = key_rows.reshape(key_rows.shape[0], heads, DH)
    product = jnp.einsum(
        "rkgd,nkd->rkgn", query_four, key_three, preferred_element_type=jnp.float32
    )
    return product * DH ** (-0.5)


def visible(query_pos, key_pos, key_live):
    return (key_live[None, :] & (key_pos[None, :] <= query_pos[:, None]))[:, None, None, :]


def masked_max(scores, seen):
    return jnp.max(jnp.where(seen, scores, NEGATIVE), axis=-1)


def weights_of(scores, seen, top):
    return jnp.where(seen, jnp.exp(scores - top[..., None]), 0.0)


def accumulate(weights, value_rows):
    heads = value_rows.shape[1] // DH
    value_three = value_rows.reshape(value_rows.shape[0], heads, DH)
    return jnp.einsum(
        "rkgn,nkd->rkgd",
        weights.astype(jnp.bfloat16),
        value_three,
        preferred_element_type=jnp.float32,
    )


def on_device(queries, new_keys, new_values, cache_keys, cache_values, valid_len, block_of):
    here = jnp.reshape(lax.axis_index("seq"), (1,))
    rows_here = queries.shape[0]
    length = cache_keys.shape[0]
    heads = new_keys.shape[1] // DH
    own_block = lookup(block_of, here)[0]
    span_k, span_v = sent_together((new_keys, new_values), "seq", 0, 1)
    total = span_k.shape[0]
    every = jnp.arange(total, dtype=jnp.int32)
    span_pos = lookup(block_of, every // rows_here) * rows_here + every % rows_here
    own_pos = own_block * rows_here + jnp.arange(rows_here, dtype=jnp.int32)
    start_state = (
        jnp.full((rows_here, heads, GROUP), NEGATIVE, jnp.float32),
        jnp.zeros((rows_here, heads, GROUP, DH), jnp.float32),
        jnp.zeros((rows_here, heads, GROUP), jnp.float32),
    )
    pieces = (
        lax.all_gather(cache_keys, "seq", axis=0, tiled=True),
        lax.all_gather(cache_values, "seq", axis=0, tiled=True),
    )
    count = pieces[0].shape[0]
    many = count // length

    def inner(state, item):
        key_block, value_block, first = item
        shard = first // length
        block_k = lax.dynamic_slice_in_dim(span_k, shard * rows_here, rows_here, 0)
        block_v = lax.dynamic_slice_in_dim(span_v, shard * rows_here, rows_here, 0)
        block_pos = lax.dynamic_slice_in_dim(span_pos, shard * rows_here, rows_here, 0)
        filled = lookup(valid_len, jnp.reshape(shard, (1,)))[0]
        cache_live = jnp.arange(length, dtype=jnp.int32) < filled
        cache_seen = jnp.broadcast_to(cache_live[None, None, None, :], (rows_here, 1, 1, length))
        block_seen = visible(own_pos, block_pos, jnp.ones((rows_here,), bool))
        seen = jnp.concatenate([cache_seen, block_seen], -1)
        keys = jnp.concatenate([key_block, block_k], 0)
        values = jnp.concatenate([value_block, block_v], 0)
        scores = scores_of(queries, keys)
        local = masked_max(scores, seen)
        weights = weights_of(scores, seen, local)
        part_numer = accumulate(weights, values)
        part_total = jnp.sum(weights, axis=-1)
        best, sums, totals = state
        newest = jnp.maximum(best, local)
        keep = jnp.exp(best - newest)
        fresh = jnp.exp(local - newest)
        sums = sums * keep[..., None] + part_numer * fresh[..., None]
        totals = totals * keep + part_total * fresh
        return ((newest, sums, totals), None)

    firsts = length * jnp.arange(many, dtype=jnp.int32)
    state, _ = lax.scan(
        inner,
        start_state,
        (pieces[0].reshape(many, length, -1), pieces[1].reshape(many, length, -1), firsts),
    )
    final_top, numer, denom = state
    result = numer / denom[..., None]
    return result.reshape(rows_here, -1).astype(jnp.bfloat16)


def solution(mesh):
    placed = (
        P(("groups", "seq"), "head"),
        P(("groups", "seq"), "head"),
        P(("groups", "seq"), "head"),
        P(("groups", "seq"), "head"),
        P(("groups", "seq"), "head"),
        P("groups"),
        P("groups"),
    )
    return jax.shard_map(
        on_device,
        mesh=mesh,
        in_specs=placed,
        out_specs=P(("groups", "seq"), "head"),
        check_vma=False,
    )
```

profile of v0, /device:TPU:513, one launch (start us, length us, event | category | flops | bytes accessed | tf_op | source)
XLA Modules:
  0.0 292.7 jit_solution(12681562831767876139)
XLA Ops:
  9.0 1.3 broadcast_in_dim.92
  10.3 23.9 %all-to-all-start = ((bf16[16,128,256]{1,2,0:T(8,128)(2,1)}), bf16[16,128,256]{1,2,0:T(8,128)(2,1)S(1)}, u32[]{:S(2)}, u32[]{:S(2)}) async-start(bf16[16,128,256]{1,2,0:T(8,128)(2,1)} %broadcast_in_dim.92), calls=%async_computation | async-start | bytes 2097152 | tf_op jit(solution)/shard_map/all_to_all | solution.py:19
  34.2 1.4 fusion.47
  37.0 32.5 %all-to-all-done = bf16[16,128,256]{1,2,0:T(8,128)(2,1)S(1)} async-done(((bf16[16,128,256]{1,2,0:T(8,128)(2,1)}), bf16[16,128,256]{1,2,0:T(8,128)(2,1)S(1)}, u32[]{:S(2)}, u32[]{:S(2)}) %all-to-all-start) | async-done | bytes 1048608 | tf_op jit(solution)/shard_map/all_to_all | solution.py:19
  70.1 15.4 %all-gather.3.cloned.1.call-done = bf16[16384,128]{1,0:T(8,128)(2,1)} async-done(((bf16[1024,128]{1,0:T(8,128)(2,1)}), bf16[16384,128]{1,0:T(8,128)(2,1)}) %all-gather.3.cloned.1.call-update) | async-done | bytes 4194320 | tf_op jit(solution)/shard_map/all_gather | solution.py:92
  85.5 45.5 %all-gather.5.cloned.1.call-done = bf16[16384,128]{1,0:T(8,128)(2,1)} async-done(((bf16[1024,128]{1,0:T(8,128)(2,1)}), bf16[16384,128]{1,0:T(8,128)(2,1)}) %all-gather.5.cloned.1.call-update) | async-done | bytes 4194320 | tf_op jit(solution)/shard_map/all_gather | solution.py:93
  131.0 153.9 %while.17 = (s32[]{:T(128)}, f32[128,1,8]{0,2,1:T(8,128)S(1)}, f32[128,1,8,128]{0,3,2,1:T(8,128)S(1)}, f32[128,1,8]{0,2,1:T(8,128)S(1)}, s32[16]{0:T(128)S(1)}, ...) while((s32[]{:T(128)}, f32[128,1,8]{0,2,1:T(8,128)S(1)}, ...), condition=%wide.region_6.7_spmd.clone, body=%wide.region_2.6_spmd.clone.sunk | while | flops 616474816 | bytes 18533632 | solution.py:125
  139.5 1.1 fusion.65
  149.2 1.1 fusion.65
  155.0 1.0 constant_dynamic-slice_fusion.6
  158.8 1.1 fusion.65
  168.4 1.1 fusion.65
  178.0 1.1 fusion.65
  187.6 1.1 fusion.65
  197.3 1.1 fusion.65
  206.9 1.1 fusion.65
  216.5 1.1 fusion.65
  226.1 1.1 fusion.65
  235.8 1.1 fusion.65
  245.4 1.1 fusion.65
  255.0 1.1 fusion.65
  264.6 1.1 fusion.65
  274.2 1.1 fusion.65
  283.9 1.1 fusion.65
  (308 shorter events, 101.1 us)
Async XLA Ops:
  6.5 124.5 %copy-start.1 = (s32[16]{0:T(128)S(1)}, s32[16]{0:T(128)}, u32[]{:S(2)}) copy-start(s32[16]{0:T(128)} %param.14) | copy-start | bytes 196
  6.5 124.5 %copy-start = (bf16[128,1024]{1,0:T(8,128)(2,1)S(1)}, bf16[128,1024]{1,0:T(8,128)(2,1)}, u32[]{:S(2)}) copy-start(bf16[128,1024]{1,0:T(8,128)(2,1)} %param.9) | copy-start | bytes 786436
  6.6 78.9 %all-gather.3.cloned.1.call-start = ((), (), s32[]{:S(2)}) async-start(), calls=%async_computation.1 | async-start | bytes 4456448 | tf_op jit(solution)/shard_map/all_gather | solution.py:92
  7.3 123.7 %all-gather.5.cloned.1.call-start = ((), (), s32[]{:S(2)}) async-start(), calls=%async_computation.2 | async-start | bytes 4456448 | tf_op jit(solution)/shard_map/all_gather | solution.py:93
  10.3 59.2 %all-to-all-start = ((bf16[16,128,256]{1,2,0:T(8,128)(2,1)}), bf16[16,128,256]{1,2,0:T(8,128)(2,1)S(1)}, u32[]{:S(2)}, u32[]{:S(2)}) async-start(bf16[16,128,256]{1,2,0:T(8,128)(2,1)} %broadcast_in_dim.92), calls=%async_computation | async-start | bytes 2097152 | tf_op jit(solution)/shard_map/all_to_all | solution.py:19
Sparse Core Ops, SparseCore 0:
  9.2 76.2 all-gather.2
  87.3 43.6 all-gather.4
where the time goes:
time: 295 us; the launch traced here: 293 us
  waiting for transfers between devices  94.9 us (32%)
  local copies, waits for them, and re-layouts  49.1 us (17%)
  other arithmetic  40.9 us (14%)
  loops' own time  39 us (13%)
  matrix products  30.6 us (10%)
  starting transfers between devices  23.9 us (8%)
  between operations  14.2 us (5%)
    all_gather x1, waiting for transfers between devices, on_device(): lax.all_gather(cache_values, 'seq', axis=0, tiled=True)  45.5 us
    another operation x1, loops' own time, on_device(): lax.scan(inner, start_state, (pieces[0].reshape(many, length, -1), pieces...  39 us
    all_to_all x1, waiting for transfers between devices, from_everyone(): lax.all_to_all(jnp.broadcast_to(array[None], (size, *array.shape)), axis,...  32.5 us
    dynamic_slice x48, local copies, waits for them, and re-layouts, on_device(): lax.scan(inner, start_state, (pieces[0].reshape(many, length, -1), pieces...  27.4 us
    all_to_all x1, starting transfers between devices, from_everyone(): lax.all_to_all(jnp.broadcast_to(array[None], (size, *array.shape)), axis,...  23.9 us
    dot_general x16, matrix products, accumulate(): jnp.einsum('rkgn,nkd->rkgd', weights.astype(jnp.bfloat16), value_three, p...  17.5 us
    squeeze x16, local copies, waits for them, and re-layouts, on_device(): lax.scan(inner, start_state, (pieces[0].reshape(many, length, -1), pieces...  15.6 us
    all_gather x1, waiting for transfers between devices, on_device(): lax.all_gather(cache_keys, 'seq', axis=0, tiled=True)  15.4 us
  transfers between devices with their start and end apart: 3, of which 3 were waited for; matrix products, arithmetic and copies ran while one was open for 2% of the time, Pallas kernels for 0%

commit v1 on v0

--- a/solution.py
+++ b/solution.py
@@ -89,7 +89,9 @@
         jnp.zeros((rows_here, heads, GROUP), jnp.float32),
     )
     pieces = (
-        lax.all_gather(cache_keys, "seq", axis=0, tiled=True),
+        jnp.concatenate(
+            lax.all_to_all(jnp.stack([cache_keys] * lax.axis_size("seq")), "seq", 0, 0), axis=0
+        ),
         lax.all_gather(cache_values, "seq", axis=0, tiled=True),
     )
     count = pieces[0].shape[0]

time: 295 us -> 335 us (1.14)
  waiting for transfers between devices: 94.9 us -> 128 us
  starting transfers between devices: 23.9 us -> 29.2 us
  local copies, waits for them, and re-layouts: 49.1 us -> 52.8 us
    all_to_all x0 -> x1, waiting for transfers between devices: none -> 60.7 us  [on_device(): lax.all_to_all(jnp.stack([cache_keys] * lax.axis_size('seq')), 'seq', 0, 0)]
    all_gather x1 -> x0, waiting for transfers between devices: 15.4 us -> none  [on_device(): lax.all_gather(cache_keys, 'seq', axis=0, tiled=True)]
    all_gather x1, waiting for transfers between devices: 45.5 us -> 36.9 us  [on_device(): lax.all_gather(cache_values, 'seq', axis=0, tiled=True)]
    all_to_all x0 -> x1, starting transfers between devices: none -> 5.27 us  [on_device(): lax.all_to_all(jnp.stack([cache_keys] * lax.axis_size('seq')), 'seq', 0, 0)]
    another operation x0 -> x1, local copies, waits for them, and re-layouts: none -> 3.72 us  [on_device(): jnp.stack([cache_keys] * lax.axis_size('seq'))]
where the time goes in v1:
time: 335 us; the launch traced here: 333 us
  waiting for transfers between devices  128 us (38%)
  local copies, waits for them, and re-layouts  52.8 us (16%)
  other arithmetic  39.6 us (12%)
  loops' own time  39 us (12%)
  matrix products  30.6 us (9%)
  starting transfers between devices  29.2 us (9%)
  between operations  14.1 us (4%)
    all_to_all x1, waiting for transfers between devices, on_device(): lax.all_to_all(jnp.stack([cache_keys] * lax.axis_size('seq')), 'seq', 0, 0)  60.7 us
    another operation x1, loops' own time, on_device(): lax.scan(inner, start_state, (pieces[0].reshape(many, length, -1), pieces...  39 us
    all_gather x1, waiting for transfers between devices, on_device(): lax.all_gather(cache_values, 'seq', axis=0, tiled=True)  36.9 us
    all_to_all x1, waiting for transfers between devices, from_everyone(): lax.all_to_all(jnp.broadcast_to(array[None], (size, *array.shape)), axis,...  29.2 us
    dynamic_slice x48, local copies, waits for them, and re-layouts, on_device(): lax.scan(inner, start_state, (pieces[0].reshape(many, length, -1), pieces...  27.4 us
    all_to_all x1, starting transfers between devices, from_everyone(): lax.all_to_all(jnp.broadcast_to(array[None], (size, *array.shape)), axis,...  23.9 us
    dot_general x16, matrix products, accumulate(): jnp.einsum('rkgn,nkd->rkgd', weights.astype(jnp.bfloat16), value_three, p...  17.5 us
    squeeze x16, local copies, waits for them, and re-layouts, on_device(): lax.scan(inner, start_state, (pieces[0].reshape(many, length, -1), pieces...  15.6 us
  transfers between devices with their start and end apart: 3, of which 3 were waited for; matrix products, arithmetic and copies ran while one was open for 2% of the time, Pallas kernels for 0%

profile of v1, /device:TPU:513, one launch (start us, length us, event | category | flops | bytes accessed | tf_op | source)
XLA Modules:
  0.0 333.0 jit_solution(12316980330915372116)
XLA Ops:
  7.4 1.2 broadcast_in_dim.92
  8.6 23.9 %all-to-all-start.1 = ((bf16[16,128,256]{1,2,0:T(8,128)(2,1)}), bf16[16,128,256]{1,2,0:T(8,128)(2,1)S(1)}, u32[]{:S(2)}, u32[]{:S(2)}) async-start(bf16[16,128,256]{1,2,0:T(8,128)(2,1)} %broadcast_in_dim.92), calls=%async_computation.1 | async-start | bytes 2097152 | tf_op jit(solution)/shard_map/all_to_all | solution.py:19
  33.3 29.2 %all-to-all-done.1 = bf16[16,128,256]{1,2,0:T(8,128)(2,1)S(1)} async-done(((bf16[16,128,256]{1,2,0:T(8,128)(2,1)}), bf16[16,128,256]{1,2,0:T(8,128)(2,1)S(1)}, u32[]{:S(2)}, u32[]{:S(2)}) %all-to-all-start.1) | async-done | bytes 1048608 | tf_op jit(solution)/shard_map/all_to_all | solution.py:19
  62.5 3.7 %stack.2 = bf16[16,1024,128]{2,1,0:T(8,128)(2,1)} broadcast(bf16[1024,128]{1,0:T(8,128)(2,1)} %param.12), dimensions={1,2} | broadcast | bytes 4456448 | tf_op jit(solution)/shard_map/stack | solution.py:93
  66.2 5.3 %all-to-all-start = ((bf16[16,1024,128]{2,1,0:T(8,128)(2,1)}), bf16[16,1024,128]{2,1,0:T(8,128)(2,1)}, u32[]{:S(2)}, u32[]{:S(2)}) async-start(bf16[16,1024,128]{2,1,0:T(8,128)(2,1)} %stack.2), calls=%async_computation | async-start | bytes 8388608 | tf_op jit(solution)/shard_map/all_to_all | solution.py:93
  73.6 36.9 %all-gather.2.cloned.1.call-done = bf16[16384,128]{1,0:T(8,128)(2,1)} async-done(((bf16[1024,128]{1,0:T(8,128)(2,1)}), bf16[16384,128]{1,0:T(8,128)(2,1)}) %all-gather.2.cloned.1.call-update) | async-done | bytes 4194320 | tf_op jit(solution)/shard_map/all_gather | solution.py:95
  110.5 60.7 %all-to-all-done = bf16[16,1024,128]{2,1,0:T(8,128)(2,1)} async-done(((bf16[16,1024,128]{2,1,0:T(8,128)(2,1)}), bf16[16,1024,128]{2,1,0:T(8,128)(2,1)}, u32[]{:S(2)}, u32[]{:S(2)}) %all-to-all-start) | async-done | bytes 4194336 | tf_op jit(solution)/shard_map/all_to_all | solution.py:93
  171.3 153.9 %while.17 = (s32[]{:T(128)}, f32[128,1,8]{0,2,1:T(8,128)S(1)}, f32[128,1,8,128]{0,3,2,1:T(8,128)S(1)}, f32[128,1,8]{0,2,1:T(8,128)S(1)}, s32[16]{0:T(128)S(1)}, ...) while((s32[]{:T(128)}, f32[128,1,8]{0,2,1:T(8,128)S(1)}, ...), condition=%wide.region_6.7_spmd.clone, body=%wide.region_2.6_spmd.clone.sunk | while | flops 616474816 | bytes 18533632 | solution.py:127
  179.8 1.1 fusion.65
  189.4 1.1 fusion.65
  199.0 1.1 fusion.65
  208.7 1.1 fusion.65
  218.3 1.1 fusion.65
  227.9 1.1 fusion.65
  237.5 1.1 fusion.65
  247.1 1.1 fusion.65
  256.8 1.1 fusion.65
  266.4 1.1 fusion.65
  276.0 1.1 fusion.65
  285.6 1.1 fusion.65
  295.2 1.1 fusion.65
  304.9 1.1 fusion.65
  314.5 1.1 fusion.65
  324.1 1.1 fusion.65
  (310 shorter events, 101.4 us)
Async XLA Ops:
  8.6 53.9 %all-to-all-start.1 = ((bf16[16,128,256]{1,2,0:T(8,128)(2,1)}), bf16[16,128,256]{1,2,0:T(8,128)(2,1)S(1)}, u32[]{:S(2)}, u32[]{:S(2)}) async-start(bf16[16,128,256]{1,2,0:T(8,128)(2,1)} %broadcast_in_dim.92), calls=%async_computation.1 | async-start | bytes 2097152 | tf_op jit(solution)/shard_map/all_to_all | solution.py:19
  32.5 78.0 %all-gather.2.cloned.1.call-start = ((), (), s32[]{:S(2)}) async-start(), calls=%async_computation.2 | async-start | bytes 4456448 | tf_op jit(solution)/shard_map/all_gather | solution.py:95
  66.2 5.3 %copy-start = (s32[16]{0:T(128)S(1)}, s32[16]{0:T(128)}, u32[]{:S(2)}) copy-start(s32[16]{0:T(128)} %param.15) | copy-start | bytes 196
  66.2 105.0 %copy-start.1 = (bf16[128,1024]{1,0:T(8,128)(2,1)S(1)}, bf16[128,1024]{1,0:T(8,128)(2,1)}, u32[]{:S(2)}) copy-start(bf16[128,1024]{1,0:T(8,128)(2,1)} %param.9) | copy-start | bytes 786436
  66.2 105.0 %copy-start.2 = (s32[16]{0:T(128)S(1)}, s32[16]{0:T(128)}, u32[]{:S(2)}) copy-start(s32[16]{0:T(128)} %param.14) | copy-start | bytes 196
  66.2 105.0 %all-to-all-start = ((bf16[16,1024,128]{2,1,0:T(8,128)(2,1)}), bf16[16,1024,128]{2,1,0:T(8,128)(2,1)}, u32[]{:S(2)}, u32[]{:S(2)}) async-start(bf16[16,1024,128]{2,1,0:T(8,128)(2,1)} %stack.2), calls=%async_computation | async-start | bytes 8388608 | tf_op jit(solution)/shard_map/all_to_all | solution.py:93
Sparse Core Ops, SparseCore 0:
  35.2 75.3 all-gather.1
